TPU v7x, 32 devices: a whole 2x2x4 slice. The times are simulated.
32 devices in a mesh: m: 2 (over x), kk: 4 (over z), g: 4 (over y, core).
Axes of the slice: x: 2, y: 2, z: 4, core: 2. Of those that a mesh axis runs over, the one named last changes fastest.
Arguments:
- a_mat: bfloat16 [16384, 28672], P(('m', 'g'), 'kk'), parts along dimension 0
Outputs:
- output: float32 [8, 3, 2048, 2048], P(('m', 'g'), None, 'kk'), parts along dimension 0
There are 2 independent parts. A program takes and returns all parts, laid end to end along the dimension named above; each array names one.
All inputs are finite; a program needn't handle non-finite values.
Results may differ from a plain program's by a relative error of at most 0.001.
Values are sent between devices in bfloat16 or wider.
A program may use at most 1 GiB of HBM per device.

v0:
```python
import math
import jax
import jax.numpy as jnp
from jax import lax
from jax.sharding import PartitionSpec as P


def block_offsets(groups):
    half_size = groups // 2
    step_width = max(1, math.isqrt(half_size))
    big_count = -(-half_size // step_width)
    small_offs = [step_width - 1 - pos_idx for pos_idx in range(step_width)]
    big_offs = [(pos_idx + 1) * step_width for pos_idx in range(big_count)]
    return half_size, small_offs, big_offs


def solution(mesh):
    groups = mesh.shape["g"]
    half_size, small_offs, big_offs = block_offsets(groups)
    has_empty = 2 * half_size == groups

    def fetch_block(a_blk, offset):
        if offset == 0:
            return a_blk
        perm_pairs = [((dest_pos + offset) % groups, dest_pos) for dest_pos in range(groups)]
        return lax.ppermute(a_blk, "g", perm_pairs)

    def local_fn(a_blk):
        dev_pos = lax.axis_index("g")
        rows_blk = a_blk.shape[0]
        small_stack = jnp.stack([fetch_block(a_blk, offset) for offset in small_offs])
        big_stack = jnp.stack([fetch_block(a_blk, offset) for offset in big_offs])
        diag_blk = lax.dot_general(a_blk, a_blk, (((1,), (1,)), ((), ())), preferred_element_type=jnp.float32)
        cross_blk = jnp.einsum("jrk,isk->jirs", big_stack, small_stack, preferred_element_type=jnp.float32)
        cross_blk = cross_blk.reshape(-1, rows_blk, rows_blk)[:half_size]
        result = jnp.concatenate([diag_blk[None], cross_blk], axis=0)
        if has_empty:
            slot_ids = jnp.arange(half_size + 1)[:, None, None]
            result = jnp.where((slot_ids == half_size) & (dev_pos >= half_size), 0.0, result)
        result = lax.psum_scatter(result, "kk", scatter_dimension=1, tiled=True)
        return result[None]

    return jax.shard_map(local_fn, mesh=mesh, in_specs=(P(("m", "g"), "kk"),), out_specs=P(("m", "g"), None, "kk", None), check_vma=False)
```

profile of v0, /device:TPU:0, one launch (start us, length us, event | category | flops | bytes accessed | tf_op | source)
XLA Modules:
  0.0 1948.7 jit_solution(15441492752607192053)
XLA Ops:
  6.5 0.0 reduce-scatter.2.cloned.1.call-start
  6.5 2.5 collective-permute-start
  9.0 0.6 collective-permute-start.1
  9.6 0.5 compare_and_fusion
  10.1 70.1 %convolution_bitcast_fusion = f32[1,2048,2048]{2,1,0:T(8,128)} fusion(bf16[2048,7168]{1,0:T(8,128)(2,1)} %param.1), kind=kOutput, calls=%fused_computation.6 | convolution fusion | flops 60129542144 | bytes 46137344 | tf_op jit(solution)/shard_map/dot_general | solution.py:33
  80.2 559.0 %collective-permute-done = bf16[2048,7168]{1,0:T(8,128)(2,1)} collective-permute-done((bf16[2048,7168]{1,0:T(8,128)(2,1)}, bf16[2048,7168]{1,0:T(8,128)(2,1)}, u32[]{:S(2)}, u32[]{:S(2)}) %collective-permute-start) | collective-permute-done | bytes 29360160 | tf_op jit(solution)/shard_map/ppermute | solution.py:26
  639.1 315.6 %collective-permute-done.1 = bf16[2048,7168]{1,0:T(8,128)(2,1)} collective-permute-done((bf16[2048,7168]{1,0:T(8,128)(2,1)}, bf16[2048,7168]{1,0:T(8,128)(2,1)}, u32[]{:S(2)}, u32[]{:S(2)}) %collective-permute-start.1) | collective-permute-done | bytes 29360160 | tf_op jit(solution)/shard_map/ppermute | solution.py:26
  954.7 0.0 copy-start
  954.7 132.8 %fusion = f32[2,2048,2048]{2,1,0:T(8,128)} fusion(bf16[1,2048,7168]{2,1,0:T(8,128)(2,1)} %bitcast.2, bf16[1,2048,7168]{2,1,0:T(8,128)(2,1)} %bitcast.1, bf16[2048,7168]{1,0:T(8,128)(2,1)} %param.1), kind=kOutput, calls=%fused_computation | convolution fusion | flops 120288444416 | bytes 121634816 | tf_op jit(solution)/shard_map/jrk,isk->jirs/dot_general | solution.py:34
  1087.5 0.0 copy-done
  1087.5 34.5 %maximum_select_fusion = f32[3,2048,2048]{2,1,0:T(8,128)} fusion(f32[2,2048,2048]{2,1,0:T(8,128)} %fusion, f32[1,2048,2048]{2,1,0:T(8,128)} %convolution_bitcast_fusion, pred[3]{0:T(512)(128)(4,1)S(1)} %copy-done), kind=kLoop, calls=%fused_computation.4 | loop fusion | flops 25165824 | bytes 100663296 | tf_op jit(solution)/shard_map/jit(_where)/select_n | solution.py:39
  1122.0 0.0 reduce-scatter.2.cloned.1.call-update
  1122.0 819.8 %reduce-scatter.2.cloned.1.call-done = f32[3,512,2048]{2,1,0:T(8,128)} async-done(((f32[3,2048,2048]{2,1,0:T(8,128)}), f32[3,512,2048]{2,1,0:T(8,128)}) %reduce-scatter.2.cloned.1.call-update) | async-done | bytes 12582928 | tf_op jit(solution)/shard_map/reduce_scatter | solution.py:40
Async XLA Ops:
  6.5 1935.3 %reduce-scatter.2.cloned.1.call-start = ((), (), s32[]{:S(2)}) async-start(), calls=%async_computation.1 | async-start | bytes 62914560 | tf_op jit(solution)/shard_map/reduce_scatter | solution.py:40
  6.5 632.6 %collective-permute-start = (bf16[2048,7168]{1,0:T(8,128)(2,1)}, bf16[2048,7168]{1,0:T(8,128)(2,1)}, u32[]{:S(2)}, u32[]{:S(2)}) collective-permute-start(bf16[2048,7168]{1,0:T(8,128)(2,1)} %param.1), channel_id=1, source_target_pairs={{1,0},{2,1},{3,2},{0,3},{5,4},{6,5},{7,6},{4,7},{9,8},{10,9},{11,1... | collective-permute-start | bytes 88080392 | tf_op jit(solution)/shard_map/ppermute | solution.py:26
  9.0 945.7 %collective-permute-start.1 = (bf16[2048,7168]{1,0:T(8,128)(2,1)}, bf16[2048,7168]{1,0:T(8,128)(2,1)}, u32[]{:S(2)}, u32[]{:S(2)}) collective-permute-start(bf16[2048,7168]{1,0:T(8,128)(2,1)} %param.1), channel_id=1, source_target_pairs={{2,0},{3,1},{0,2},{1,3},{6,4},{7,5},{4,6},{5,7},{10,8},{11,9},{8,1... | collective-permute-start | bytes 88080392 | tf_op jit(solution)/shard_map/ppermute | solution.py:26
  954.7 132.8 %copy-start = (pred[3]{0:T(512)(128)(4,1)S(1)}, pred[3]{0:T(512)(128)(4,1)}, u32[]{:S(2)}) copy-start(pred[3]{0:T(512)(128)(4,1)} %compare_and_fusion) | copy-start | bytes 13
Sparse Core Ops, SparseCore 0:
  1122.2 819.6 reduce-scatter.1
where the time goes:
time: 1950 us
  waiting for transfers between devices  1690 us (87%)
  matrix products  203 us (10%)
  other arithmetic  35 us (2%)
    ppermute x2, waiting for transfers between devices, fetch_block(): return lax.ppermute(a_blk, 'g', perm_pairs)  875 us
    reduce_scatter x1, waiting for transfers between devices, local_fn(): result = lax.psum_scatter(result, 'kk', scatter_dimension=1, tiled=True)  820 us
    dot_general x1, matrix products, local_fn(): jnp.einsum('jrk,isk->jirs', big_stack, small_stack, preferred_element_typ...  133 us
    dot_general x1, matrix products, local_fn(): lax.dot_general(a_blk, a_blk, (((1,), (1,)), ((), ())), preferred_element...  70.1 us
  transfers between devices with their start and end apart: 3, of which 3 were waited for; matrix products, arithmetic and copies ran while one was open for 4% of the time, Pallas kernels for 0%

commit v1 on v0

v1 whole, which is shorter than its diff:
```python
import jax
import jax.numpy as jnp
from jax import lax
from jax.experimental import pallas as pl
from jax.experimental.pallas import tpu as pltpu
from jax.sharding import PartitionSpec as P


PIECES = ((1, 3), (2,), (1,), (1,))
CHIP_SWAP = [(0, 1), (1, 0), (2, 3), (3, 2)]
CROSS = [(0, 3), (1, 2), (2, 0), (3, 1)]
DEPTH = 3584
VMEM = 60 * 1024 * 1024
ANY = pl.BlockSpec(memory_space=pl.ANY)


def dot_t(left, right):
    return lax.dot_general(left, right, (((1,), (1,)), ((), ())), preferred_element_type=jnp.float32)


def mm(load_l, load_r, cols, acc):
    acc[...] = jnp.zeros_like(acc)

    def step(k, _):
        ks = pl.ds(pl.multiple_of(k * DEPTH, DEPTH), DEPTH)
        acc[...] += dot_t(load_l(ks), load_r(ks))
        return 0

    lax.fori_loop(0, cols // DEPTH, step, 0)


def cost(m, n, k):
    return pl.CostEstimate(flops=2 * m * n * k, bytes_accessed=2 * (m + n) * k + 4 * m * n, transcendentals=0)


def params(n):
    return pltpu.CompilerParams(vmem_limit_bytes=VMEM, dimension_semantics=("arbitrary",) * n)


def same_call(a, zs):
    rows, cols = a.shape
    q = rows // zs

    def body(a_ref, o_ref):
        mm(lambda ks: a_ref[:, ks], lambda ks: a_ref[:, ks], cols, o_ref.at[0])

    return pl.pallas_call(
        body,
        grid=(zs,),
        in_specs=[pl.BlockSpec((q, cols), lambda r: (r, 0))],
        out_specs=pl.BlockSpec((1, q, q), lambda r: (r, 0, 0)),
        out_shape=jax.ShapeDtypeStruct((zs, q, q), jnp.float32),
        compiler_params=params(1),
        cost_estimate=cost(rows, q, cols),
        name="same_block",
    )(a)


def rest_call(a, dep, zs):
    rows, cols = a.shape
    q = rows // zs
    h = q // 2

    def body(l_ref, r_ref, dep_ref, o_ref):
        mm(lambda ks: l_ref[:, ks], lambda ks: r_ref[:, ks], cols, o_ref.at[0])

    def left(r, c):
        return (jnp.where((c == 2) & (r >= 2), r - 2, r), 0)

    def right(r, c):
        far = jnp.where(r < 2, 2 * (r + 2), 2 * r + 1)
        return (jnp.where(c == 2, far, 2 * ((r + 3) % 4) + c), 0)

    return pl.pallas_call(
        body,
        grid=(zs, 3),
        in_specs=[pl.BlockSpec((q, cols), left), pl.BlockSpec((h, cols), right), ANY],
        out_specs=pl.BlockSpec((1, q, h), lambda r, c: (r, 0, c)),
        out_shape=jax.ShapeDtypeStruct((zs, q, 3 * h), jnp.float32),
        compiler_params=params(2),
        cost_estimate=cost(rows, 3 * h, cols),
        name="rest_block",
    )(a, a, dep)


def near_call(left, right, which, dep, zs):
    rows, cols = left.shape
    h = rows // zs // 2

    def body(l_ref, r_ref, dep_ref, o_ref):
        mm(lambda ks: l_ref[:, 0, :, ks].reshape(zs * h, -1), lambda ks: r_ref[:, ks], cols, o_ref)

    return pl.pallas_call(
        body,
        grid=(rows // h,),
        in_specs=[
            pl.BlockSpec((zs, 1, h, cols), lambda j: (0, which, 0, 0), pipeline_mode=pl.Buffered(1)),
            pl.BlockSpec((h, cols), lambda j: (j, 0)),
            ANY,
        ],
        out_specs=pl.BlockSpec((zs * h, h), lambda j: (0, j)),
        out_shape=jax.ShapeDtypeStruct((zs * h, rows), jnp.float32),
        compiler_params=params(1),
        cost_estimate=cost(zs * h, rows, cols),
        name="near_block",
    )(left.reshape(zs, 2, h, cols), right, dep)


def cross_call(pos, gots, a, dep, zs):
    rows, cols = a.shape
    q = rows // zs
    sizes = [x.shape[0] // zs for x in gots]
    n = sum(sizes)

    def body(pos_ref, *refs):
        l_refs, (r_ref, dep_ref, o_ref, acc) = refs[: len(sizes)], refs[len(sizes) :]
        j = pl.program_id(0)
        lo = 0
        for l_ref, size in zip(l_refs, sizes):
            part = acc.at[:, : zs * size]
            mm(lambda ks: r_ref[:, ks], lambda ks: l_ref[:, ks], cols, part)

            @pl.when(pos_ref[0] != 2)
            def _():
                prod = part[...].T
                for s in range(zs):
                    o_ref[s, lo : lo + size, pl.ds(pl.multiple_of(j * q, q), q)] = prod[s * size : (s + 1) * size]

            @pl.when(pos_ref[0] == 2)
            def _():
                prod = part[...].T
                for s in range(zs):
                    o_ref[j, lo : lo + size, s * q : (s + 1) * q] = prod[s * size : (s + 1) * size]

            lo += size

    return pl.pallas_call(
        body,
        grid_spec=pltpu.PrefetchScalarGridSpec(
            num_scalar_prefetch=1,
            grid=(zs,),
            in_specs=[pl.BlockSpec(x.shape, lambda j, p: (0, 0), pipeline_mode=pl.Buffered(1)) for x in gots]
            + [pl.BlockSpec((q, cols), lambda j, p: (j, 0)), ANY],
            out_specs=pl.BlockSpec((zs, n, rows), lambda j, p: (0, 0, 0)),
            scratch_shapes=[pltpu.VMEM((q, zs * max(sizes)), jnp.float32)],
        ),
        out_shape=jax.ShapeDtypeStruct((zs, n, rows), jnp.float32),
        compiler_params=params(1),
        cost_estimate=cost(zs * n, rows, cols),
        name="cross_block",
    )(pos, *gots, a, dep)


def own_call(zpos, same, low, up, far, far_other, rows):
    q = same.shape[0]

    def body(z_ref, same_ref, low_ref, up_ref, far_ref, other_ref, o_ref):
        z = z_ref[0]

        def cols(rel):
            return pl.ds(pl.multiple_of(((z + rel) % 4) * q, q), q)

        o_ref[0, :, cols(0)] = same_ref[...]
        o_ref[0, :, cols(1)] = up_ref[...].T
        o_ref[0, :, cols(3)] = low_ref[...]

        @pl.when(z < 2)
        def _():
            o_ref[0, :, cols(2)] = jnp.concatenate([far_ref[...], other_ref[...]], axis=1)

        @pl.when(z >= 2)
        def _():
            o_ref[0, :, cols(2)] = jnp.concatenate([other_ref[...], far_ref[...]], axis=1).T

    whole = lambda x: pl.BlockSpec(x.shape, lambda i, z: (0, 0))
    ins = (same, low, up, far, far_other)
    return pl.pallas_call(
        body,
        grid_spec=pltpu.PrefetchScalarGridSpec(
            num_scalar_prefetch=1,
            grid=(1,),
            in_specs=[whole(x) for x in ins],
            out_specs=pl.BlockSpec((1, q, rows), lambda i, z: (0, 0, 0)),
        ),
        out_shape=jax.ShapeDtypeStruct((3, q, rows), jnp.float32),
        compiler_params=params(1),
        name="own_out",
    )(zpos, *ins)


def slots_call(pos, out, near, near_other, mine, sent):
    _, q, rows = out.shape
    spans = []
    for x in mine:
        lo = spans[-1][1] if spans else 0
        spans.append((lo, lo + x.shape[0]))
    n = len(mine)

    def body(p_ref, out_ref, near_ref, other_ref, *refs):
        mine_refs, sent_refs, o_ref, buf = refs[:n], refs[n : 2 * n], refs[2 * n], refs[2 * n + 1]
        p = p_ref[0]
        slot = pl.program_id(0) + 1

        @pl.when(((slot == 1) & (p == 3)) | ((slot == 2) & (p < 2)))
        def _():
            for (lo, hi), ref in zip(spans, mine_refs):
                o_ref[0, lo:hi, :] = ref[...]

        @pl.when((slot == 2) & (p >= 2))
        def _():
            o_ref[...] = jnp.zeros_like(o_ref)

        @pl.when((slot == 1) & (p % 2 == 0))
        def _():
            o_ref[0, : q // 2, :] = near_ref[...]
            o_ref[0, q // 2 :, :] = other_ref[...]

        @pl.when((slot == 1) & (p == 1))
        def _():
            for (lo, hi), ref in zip(spans, sent_refs):
                buf[lo:hi, :] = ref[...]
            for s in range(rows // q):
                o_ref[0, :, s * q : (s + 1) * q] = buf[:, s * q : (s + 1) * q].T

    whole = lambda x: pl.BlockSpec(x.shape, lambda i, p: (0, 0), pipeline_mode=pl.Buffered(1))
    ins = (near, near_other, *mine, *sent)
    return pl.pallas_call(
        body,
        grid_spec=pltpu.PrefetchScalarGridSpec(
            num_scalar_prefetch=1,
            grid=(2,),
            in_specs=[ANY] + [whole(x) for x in ins],
            out_specs=pl.BlockSpec((1, q, rows), lambda i, p: (i + 1, 0, 0)),
            scratch_shapes=[pltpu.VMEM((q, rows), jnp.float32)],
        ),
        out_shape=jax.ShapeDtypeStruct(out.shape, jnp.float32),
        input_output_aliases={1: 0},
        compiler_params=params(1),
        name="slots_out",
    )(pos, out, *ins)


def solution(mesh):
    assert mesh.shape["g"] == 4 and mesh.shape["kk"] == 4
    zs = 4

    def scatter(parts):
        return lax.psum_scatter(parts, "kk", scatter_dimension=0, tiled=False)

    def local_fn(a):
        pos = lax.axis_index("g").astype(jnp.int32)
        zpos = lax.axis_index("kk").astype(jnp.int32)
        pos1, zpos1 = pos.reshape(1), zpos.reshape(1)
        rows, cols = a.shape
        q = rows // zs
        h = q // 2
        a4 = a.reshape(zs, q, cols)
        unit = q // sum(map(sum, PIECES))

        arrived, start, gives = [], 0, 0
        for sizes in PIECES:
            arrived.append([])
            for n in sizes:
                piece = a4[:, start : start + n * unit].reshape(-1, cols)
                arrived[-1].append(lax.ppermute(piece, "g", CROSS))
                start += n * unit
                gives += 1
        partner = lax.ppermute(a, "g", CHIP_SWAP)

        same_part = same_call(a, zs)
        same = scatter(same_part)
        rest_part = rest_call(a, same_part, zs)
        rest = scatter(rest_part)

        even = pos % 2 == 0
        near_part = lax.cond(
            even,
            lambda: near_call(partner, a, 0, rest_part, zs),
            lambda: near_call(a, partner, 1, rest_part, zs),
        )
        near = scatter(near_part.reshape(zs, h, rows))

        mine, sent, dep = [], [], near_part
        for got in arrived:
            dep = cross_call(pos1, got, a, dep, zs)
            mine.append(scatter(dep))

        low, far = rest[:, :q], rest[:, q:]
        up = lax.ppermute(low, "kk", [(r, (r - 1) % zs) for r in range(zs)])
        far_other = lax.ppermute(far, "kk", [(r, (r + 2) % zs) for r in range(zs)])
        near_other = lax.ppermute(near, "g", [(1, 0), (3, 2)])
        for x in mine:
            sent.append(lax.ppermute(x, "g", [(2, 1)]))
        out = own_call(zpos1, same, low, up, far, far_other, rows)
        out = slots_call(pos1, out, near, near_other, mine, sent)
        return out[None]

    def step(a):
        return jax.shard_map(local_fn, mesh=mesh, in_specs=(P(("m", "g"), "kk"),), out_specs=P(("m", "g"), None, "kk", None), check_vma=False)(a)

    return step
```

time: 1950 us -> 1100 us (0.56)
  waiting for transfers between devices: 1690 us -> 817 us
  Pallas kernels: 0 us -> 225 us
  matrix products: 203 us -> 0 us
  other arithmetic: 35 us -> 0 us
  local copies, waits for them, and re-layouts: 0.01 us -> 27.3 us
    reduce_scatter x1 -> x7, waiting for transfers between devices: 820 us -> 313 us  [scatter(): return lax.psum_scatter(parts, 'kk', scatter_dimension=0, tiled=False)]
    ppermute x2 -> x13, waiting for transfers between devices: 875 us -> 502 us  [the longest x5 502 us: local_fn(): arrived[-1].append(lax.ppermute(piece, 'g', CROSS))]
    pallas_call x0 -> x9, Pallas kernels: none -> 225 us  [the longest x4 106 us: cross_call(): pl.pallas_call(body, grid_spec=pltpu.PrefetchScalarGridSpec(num_scalar_pr...]
    dot_general x2 -> x0, matrix products: 203 us -> none  [the longest x1 133 us: local_fn(): jnp.einsum('jrk,isk->jirs', big_stack, small_stack, preferred_element_typ...]
    select_n x1 -> x0, other arithmetic: 34.5 us -> none  [local_fn(): jnp.where((slot_ids == half_size) & (dev_pos >= half_size), 0.0, result)]
    slice x0 -> x5, local copies, waits for them, and re-layouts: none -> 24.1 us  [the longest x3 21 us: local_fn(): piece = a4[:, start:start + n * unit].reshape(-1, cols)]
  transfers between devices with their start and end apart: 3 -> 20, of which waited for: 3 -> 9; matrix products, arithmetic and copies ran while one was open for 4% -> 2% of each run, Pallas kernels for 0% -> 15%
where the time goes in v1:
time: 1100 us
  waiting for transfers between devices  817 us (74%)
  Pallas kernels  225 us (20%)
  local copies, waits for them, and re-layouts  27.3 us (2%)
  starting transfers between devices  15.9 us (1%)
  between operations  13.6 us (1%)
    ppermute x5, waiting for transfers between devices, local_fn(): arrived[-1].append(lax.ppermute(piece, 'g', CROSS))  502 us
    reduce_scatter x7, waiting for transfers between devices, scatter(): return lax.psum_scatter(parts, 'kk', scatter_dimension=0, tiled=False)  313 us
    pallas_call x4, Pallas kernels, cross_call(): pl.pallas_call(body, grid_spec=pltpu.PrefetchScalarGridSpec(num_scalar_pr...  106 us
    pallas_call x1, Pallas kernels, rest_call(): pl.pallas_call(body, grid=(zs, 3), in_specs=[pl.BlockSpec((q, cols), left...  42.9 us
    pallas_call x1, Pallas kernels, near_call(): pl.pallas_call(body, grid=(rows // h,), in_specs=[pl.BlockSpec((zs, 1, h,...  41.8 us
  transfers between devices with their start and end apart: 20, of which 9 were waited for; matrix products, arithmetic and copies ran while one was open for 2% of the time, Pallas kernels for 15%

profile of v1, /device:TPU:0, one launch (start us, length us, event | category | flops | bytes accessed | tf_op | source)
XLA Modules:
  0.0 1098.9 jit_solution(7137556094591338240)
XLA Ops:
  6.5 0.5 collective-permute-start.2
  7.0 9.5 slice.31
  16.6 2.6 collective-permute-start.5
  19.2 7.9 fusion
  27.1 21.1 %same_block.1.dep_ref = f32[4,512,512]{2,1,0:T(8,128)} custom-call(bf16[2048,7168]{1,0:T(8,128)(2,1)} %refs_1_.5), custom_call_target="tpu_custom_call" | custom-call | flops 15032385536 | bytes 40894464 | tf_op jit(solution)/shard_map/same_block/pallas_call | solution.py:47
  48.2 42.9 %rest_block.1 = f32[4,512,768]{2,1,0:T(8,128)} custom-call(bf16[2048,7168]{1,0:T(8,128)(2,1)} %refs_1_.5, bf16[2048,7168]{1,0:T(8,128)(2,1)} %refs_1_.5, f32[4,512,512]{2,1,0:T(8,128)} %same_block.1.dep_ref), custom_call_target="tpu_custom_call" | custom-call | flops 22548578304 | bytes 46661632 | tf_op jit(solution)/shard_map/rest_block/pallas_call | solution.py:74
  91.1 41.8 %conditional.1 = (f32[1024,2048]{1,0:T(8,128)}) conditional(s32[]{:T(128)} %convert_element_type.3, (bf16[2048,7168]{1,0:T(8,128)(2,1)}, bf16[2048,7168]{1,0:T(8,128)(2,1)}, f32[4,512,768]{2,1,0:T(8,128)}) %tuple.11, (bf16[2048,7168]{1,0:T(8,128)(2,1)}, bf16[2048,7168]{1,0:T(8,128)(2,1)}, f32[4,512,768]{2,1,0:T(8,128)}) %tuple.12), branch_computations={%region_2.3_spmd, %region_3.4_spmd} | conditional | flops 30064771072 | bytes 52428808 | solution.py:276
  91.1 41.8 %near_block.3 = f32[1024,2048]{1,0:T(8,128)} custom-call(bf16[4,2,256,7168]{3,2,1,0:T(8,128)(2,1)} %bitcast.1.l_ref, bf16[2048,7168]{1,0:T(8,128)(2,1)} %get-tuple-element.24.r_ref, f32[4,512,768]{2,1,0:T(8,128)} %get-tuple-element.25.dep_ref), custom_call_target="tpu_custom_call" | custom-call | flops 30064771072 | bytes 52428800 | tf_op jit(solution)/shard_map/cond/branch_1_fun/near_block/pallas_call | solution.py:93
  132.9 202.4 %collective-permute-done.4.refs_0_ = bf16[256,7168]{1,0:T(8,128)(2,1)} collective-permute-done((bf16[256,7168]{1,0:T(8,128)(2,1)}, bf16[256,7168]{1,0:T(8,128)(2,1)}, u32[]{:S(2)}, u32[]{:S(2)}) %collective-permute-start.4) | collective-permute-done | bytes 3670048 | tf_op jit(solution)/shard_map/ppermute | solution.py:265
  335.3 47.5 %cross_block.4.refs_2_ = f32[4,256,2048]{2,1,0:T(8,128)} custom-call(s32[1]{0:T(128)} %bitcast.2.pos_ref.p_ref, bf16[256,7168]{1,0:T(8,128)(2,1)} %collective-permute-done.4.refs_0_, bf16[768,7168]{1,0:T(8,128)(2,1)} %collective-permute-done.5.refs_1_, bf16[2048,7168]{1,0:T(8,128)(2,1)} %refs_1_.5, f32[1024,2048]{1,0:T(8,128)} %get-tuple-element.29.refs_3_), custom_call_target="tpu_custom_call" | custom-call | flops 30064771072 | bytes 52428800 | tf_op jit(solution)/shard_map/cross_block/pallas_call | solution.py:137
  382.9 0.0 reduce-scatter.12.cloned.1.call-start
  382.9 0.7 reduce-scatter.12.cloned.1.call-update
  383.6 0.0 reduce-scatter.10.cloned.1.call-start
  383.7 0.7 reduce-scatter.10.cloned.1.call-update
  384.4 0.0 reduce-scatter.16.cloned.1.call-start
  384.4 3.6 slice.32
  388.0 1.3 collective-permute-start.6
  389.3 158.9 %collective-permute-done.6.refs_0_ = bf16[512,7168]{1,0:T(8,128)(2,1)} collective-permute-done((bf16[512,7168]{1,0:T(8,128)(2,1)S(1)}, bf16[512,7168]{1,0:T(8,128)(2,1)}, u32[]{:S(2)}, u32[]{:S(2)}) %collective-permute-start.6) | collective-permute-done | bytes 7340064 | tf_op jit(solution)/shard_map/ppermute | solution.py:265
  548.2 25.7 %cross_block.5.refs_2_ = f32[4,128,2048]{2,1,0:T(8,128)} custom-call(s32[1]{0:T(128)} %bitcast.2.pos_ref.p_ref, bf16[512,7168]{1,0:T(8,128)(2,1)} %collective-permute-done.6.refs_0_, bf16[2048,7168]{1,0:T(8,128)(2,1)} %refs_1_.5, f32[4,256,2048]{2,1,0:T(8,128)} %cross_block.4.refs_2_), custom_call_target="tpu_custom_call" | custom-call | flops 15032385536 | bytes 40894464 | tf_op jit(solution)/shard_map/cross_block/pallas_call | solution.py:137
  573.9 0.0 reduce-scatter.20.cloned.1.call-start
  573.9 1.2 collective-permute-start.7
  575.2 0.1 collective-permute-start.8
  575.2 81.2 %collective-permute-done.7.refs_0_ = bf16[256,7168]{1,0:T(8,128)(2,1)S(1)} collective-permute-done((bf16[256,7168]{1,0:T(8,128)(2,1)}, bf16[256,7168]{1,0:T(8,128)(2,1)S(1)}, u32[]{:S(2)}, u32[]{:S(2)}) %collective-permute-start.7) | collective-permute-done | bytes 3670048 | tf_op jit(solution)/shard_map/ppermute | solution.py:265
  656.4 1.8 copy-done.1
  658.3 16.4 %cross_block.6.refs_2_ = f32[4,64,2048]{2,1,0:T(8,128)} custom-call(s32[1]{0:T(128)} %bitcast.2.pos_ref.p_ref, bf16[256,7168]{1,0:T(8,128)(2,1)} %copy-done.1, bf16[2048,7168]{1,0:T(8,128)(2,1)} %refs_1_.5, f32[4,128,2048]{2,1,0:T(8,128)} %cross_block.5.refs_2_), custom_call_target="tpu_custom_call" | custom-call | flops 7516192768 | bytes 35127296 | tf_op jit(solution)/shard_map/cross_block/pallas_call | solution.py:137
  674.6 59.4 %collective-permute-done.8.refs_0_ = bf16[256,7168]{1,0:T(8,128)(2,1)} collective-permute-done((bf16[256,7168]{1,0:T(8,128)(2,1)}, bf16[256,7168]{1,0:T(8,128)(2,1)}, u32[]{:S(2)}, u32[]{:S(2)}) %collective-permute-start.8) | collective-permute-done | bytes 3670048 | tf_op jit(solution)/shard_map/ppermute | solution.py:265
  734.0 16.6 %cross_block.7 = f32[4,64,2048]{2,1,0:T(8,128)} custom-call(s32[1]{0:T(128)} %bitcast.2.pos_ref.p_ref, bf16[256,7168]{1,0:T(8,128)(2,1)} %collective-permute-done.8.refs_0_, bf16[2048,7168]{1,0:T(8,128)(2,1)} %refs_1_.5, f32[4,64,2048]{2,1,0:T(8,128)} %cross_block.6.refs_2_), custom_call_target="tpu_custom_call" | custom-call | flops 7516192768 | bytes 35127296 | tf_op jit(solution)/shard_map/cross_block/pallas_call | solution.py:137
  750.6 0.0 reduce-scatter.18.cloned.1.call-start
  750.7 0.5 reduce-scatter.18.cloned.1.call-update
  751.2 0.0 reduce-scatter.8.cloned.1.call-start
  751.3 0.7 reduce-scatter.8.cloned.1.call-update
  752.0 0.8 collective-permute-start.9
  752.8 1.3 collective-permute-start.3
  754.1 35.7 %reduce-scatter.10.cloned.1.call-done = f32[1,512,768]{2,1,0:T(8,128)} async-done(((f32[4,512,768]{2,1,0:T(8,128)}), f32[1,512,768]{2,1,0:T(8,128)}) %reduce-scatter.10.cloned.1.call-update) | async-done | bytes 1572880 | tf_op jit(solution)/shard_map/reduce_scatter | solution.py:248
  789.8 1.3 slice.28.low_ref
  791.1 2.7 collective-permute-start
  793.8 1.9 slice.29.far_ref
  795.7 0.7 collective-permute-start.1
  796.3 109.8 %reduce-scatter.16.cloned.1.call-done = f32[1,128,2048]{2,1,0:T(8,128)} async-done(((f32[4,128,2048]{2,1,0:T(8,128)}), f32[1,128,2048]{2,1,0:T(8,128)}) %reduce-scatter.16.cloned.1.call-update) | async-done | bytes 1048592 | tf_op jit(solution)/shard_map/reduce_scatter | solution.py:248
  906.1 1.6 collective-permute-start.10
  907.7 46.7 %reduce-scatter.20.cloned.1.call-done = f32[1,64,2048]{2,1,0:T(8,128)} async-done(((f32[4,64,2048]{2,1,0:T(8,128)}), f32[1,64,2048]{2,1,0:T(8,128)}) %reduce-scatter.20.cloned.1.call-update) | async-done | bytes 524304 | tf_op jit(solution)/shard_map/reduce_scatter | solution.py:248
  954.4 1.5 collective-permute-start.12
  955.9 43.5 %reduce-scatter.18.cloned.1.call-done = f32[1,64,2048]{2,1,0:T(8,128)} async-done(((f32[4,64,2048]{2,1,0:T(8,128)}), f32[1,64,2048]{2,1,0:T(8,128)}) %reduce-scatter.18.cloned.1.call-update) | async-done | bytes 524304 | tf_op jit(solution)/shard_map/reduce_scatter | solution.py:248
  999.4 1.5 collective-permute-start.11
  1000.9 76.8 %reduce-scatter.8.cloned.1.call-done = f32[1,512,512]{2,1,0:T(8,128)} async-done(((f32[4,512,512]{2,1,0:T(8,128)}), f32[1,512,512]{2,1,0:T(8,128)}) %reduce-scatter.8.cloned.1.call-update) | async-done | bytes 1048592 | tf_op jit(solution)/shard_map/reduce_scatter | solution.py:248
  1077.7 4.7 own_out.1.out_ref
  1082.5 1.3 copy-done.2
  1083.8 8.2 slots_out.1
  (20 shorter events, 0.1 us)
Async XLA Ops:
  6.5 745.4 %reduce-scatter.14.cloned.1.call-start = ((), (), s32[]{:S(2)}) async-start(), calls=%async_computation.10 | async-start | bytes 10485760 | tf_op jit(solution)/shard_map/reduce_scatter | solution.py:248
  6.5 84.6 %collective-permute-start.2 = (bf16[2048,7168]{1,0:T(8,128)(2,1)}, bf16[2048,7168]{1,0:T(8,128)(2,1)}, u32[]{:S(2)}, u32[]{:S(2)}) collective-permute-start(bf16[2048,7168]{1,0:T(8,128)(2,1)} %refs_1_.5), channel_id=1, source_target_pairs={{0,1},{1,0},{2,3},{3,2},{4,5},{5,4},{6,7},{7,6},{8,9},{9,8},{10,11... | collective-permute-start | bytes 88080392 | tf_op jit(solution)/shard_map/ppermute | solution.py:268
  16.6 318.8 %collective-permute-start.5 = (bf16[768,7168]{1,0:T(8,128)(2,1)}, bf16[768,7168]{1,0:T(8,128)(2,1)}, u32[]{:S(2)}, u32[]{:S(2)}) collective-permute-start(bf16[768,7168]{1,0:T(8,128)(2,1)} %bitcast.10), channel_id=1, source_target_pairs={{0,3},{1,2},{2,0},{3,1},{4,7},{5,6},{6,4},{7,5},{8,11},{9,10},{10,... | collective-permute-start | bytes 33030152 | tf_op jit(solution)/shard_map/ppermute | solution.py:265
  27.1 308.3 %collective-permute-start.4 = (bf16[256,7168]{1,0:T(8,128)(2,1)}, bf16[256,7168]{1,0:T(8,128)(2,1)}, u32[]{:S(2)}, u32[]{:S(2)}) collective-permute-start(bf16[256,7168]{1,0:T(8,128)(2,1)} %bitcast.9), channel_id=1, source_target_pairs={{0,3},{1,2},{2,0},{3,1},{4,7},{5,6},{6,4},{7,5},{8,11},{9,10},{10,... | collective-permute-start | bytes 11010056 | tf_op jit(solution)/shard_map/ppermute | solution.py:265
  382.9 369.9 %reduce-scatter.12.cloned.1.call-start = ((), (), s32[]{:S(2)}) async-start(), calls=%async_computation.9 | async-start | bytes 10485760 | tf_op jit(solution)/shard_map/reduce_scatter | solution.py:248
  383.6 406.2 %reduce-scatter.10.cloned.1.call-start = ((), (), s32[]{:S(2)}) async-start(), calls=%async_computation.8 | async-start | bytes 7864320 | tf_op jit(solution)/shard_map/reduce_scatter | solution.py:248
  384.4 521.7 %reduce-scatter.16.cloned.1.call-start = ((), (), s32[]{:S(2)}) async-start(), calls=%async_computation.11 | async-start | bytes 5242880 | tf_op jit(solution)/shard_map/reduce_scatter | solution.py:248
  388.0 160.2 %collective-permute-start.6 = (bf16[512,7168]{1,0:T(8,128)(2,1)S(1)}, bf16[512,7168]{1,0:T(8,128)(2,1)}, u32[]{:S(2)}, u32[]{:S(2)}) collective-permute-start(bf16[512,7168]{1,0:T(8,128)(2,1)S(1)} %bitcast.24), channel_id=1, source_target_pairs={{0,3},{1,2},{2,0},{3,1},{4,7},{5,6},{6,4},{7,5},{8,11},{9,10},{10,... | collective-permute-start | bytes 22020104 | tf_op jit(solution)/shard_map/ppermute | solution.py:265
  573.9 380.5 %reduce-scatter.20.cloned.1.call-start = ((), (), s32[]{:S(2)}) async-start(), calls=%async_computation.13 | async-start | bytes 2621440 | tf_op jit(solution)/shard_map/reduce_scatter | solution.py:248
  573.9 82.5 %collective-permute-start.7 = (bf16[256,7168]{1,0:T(8,128)(2,1)}, bf16[256,7168]{1,0:T(8,128)(2,1)S(1)}, u32[]{:S(2)}, u32[]{:S(2)}) collective-permute-start(bf16[256,7168]{1,0:T(8,128)(2,1)} %bitcast.26), channel_id=1, source_target_pairs={{0,3},{1,2},{2,0},{3,1},{4,7},{5,6},{6,4},{7,5},{8,11},{9,10},{10,... | collective-permute-start | bytes 11010056 | tf_op jit(solution)/shard_map/ppermute | solution.py:265
  575.2 158.9 %collective-permute-start.8 = (bf16[256,7168]{1,0:T(8,128)(2,1)}, bf16[256,7168]{1,0:T(8,128)(2,1)}, u32[]{:S(2)}, u32[]{:S(2)}) collective-permute-start(bf16[256,7168]{1,0:T(8,128)(2,1)} %bitcast.25), channel_id=1, source_target_pairs={{0,3},{1,2},{2,0},{3,1},{4,7},{5,6},{6,4},{7,5},{8,11},{9,10},{10,... | collective-permute-start | bytes 11010056 | tf_op jit(solution)/shard_map/ppermute | solution.py:265
  656.4 1.8 copy-start.1
  750.6 248.8 %reduce-scatter.18.cloned.1.call-start = ((), (), s32[]{:S(2)}) async-start(), calls=%async_computation.12 | async-start | bytes 2621440 | tf_op jit(solution)/shard_map/reduce_scatter | solution.py:248
  751.2 326.5 %reduce-scatter.8.cloned.1.call-start = ((), (), s32[]{:S(2)}) async-start(), calls=%async_computation.7 | async-start | bytes 5242880 | tf_op jit(solution)/shard_map/reduce_scatter | solution.py:248
  752.0 330.5 %collective-permute-start.9 = (f32[256,2048]{1,0:T(8,128)}, f32[256,2048]{1,0:T(8,128)S(1)}, u32[]{:S(2)}, u32[]{:S(2)}) collective-permute-start(f32[256,2048]{1,0:T(8,128)} %bitcast.27), channel_id=1, source_target_pairs={{2,1},{6,5},{10,9},{14,13},{18,17},{22,21},{26,25},{30,29}} | collective-permute-start | bytes 6291464 | tf_op jit(solution)/shard_map/ppermute | solution.py:293
  752.8 329.7 %collective-permute-start.3 = (f32[256,2048]{1,0:T(8,128)}, f32[256,2048]{1,0:T(8,128)}, u32[]{:S(2)}, u32[]{:S(2)}) collective-permute-start(f32[256,2048]{1,0:T(8,128)} %bitcast.29), channel_id=1, source_target_pairs={{1,0},{3,2},{5,4},{7,6},{9,8},{11,10},{13,12},{15,14},{17,16},{19,... | collective-permute-start | bytes 6291464 | tf_op jit(solution)/shard_map/ppermute | solution.py:291
  791.1 286.6 %copy-start = (f32[512,512]{1,0:T(8,128)}, f32[512,512]{1,0:T(8,128)S(1)}, u32[]{:S(2)}) copy-start(f32[512,512]{1,0:T(8,128)S(1)} %slice.28.low_ref) | copy-start | bytes 3145732
  791.1 164.8 %collective-permute-start = (f32[512,512]{1,0:T(8,128)S(1)}, f32[512,512]{1,0:T(8,128)}, u32[]{:S(2)}, u32[]{:S(2)}) collective-permute-start(f32[512,512]{1,0:T(8,128)S(1)} %slice.28.low_ref), channel_id=1, source_target_pairs={{0,12},{4,0},{8,4},{12,8},{1,13},{5,1},{9,5},{13,9},{2,14},{6,2},{... | collective-permute-start | bytes 3145736 | tf_op jit(solution)/shard_map/ppermute | solution.py:289
  795.7 112.1 %collective-permute-start.1 = (f32[512,256]{1,0:T(8,128)}, f32[512,256]{1,0:T(8,128)}, u32[]{:S(2)}, u32[]{:S(2)}) collective-permute-start(f32[512,256]{1,0:T(8,128)} %slice.29.far_ref), channel_id=1, source_target_pairs={{0,8},{4,12},{8,0},{12,4},{1,9},{5,13},{9,1},{13,5},{2,10},{6,14},... | collective-permute-start | bytes 1572872 | tf_op jit(solution)/shard_map/ppermute | solution.py:290
  906.1 176.4 %collective-permute-start.10 = (f32[128,2048]{1,0:T(8,128)}, f32[128,2048]{1,0:T(8,128)}, u32[]{:S(2)}, u32[]{:S(2)}) collective-permute-start(f32[128,2048]{1,0:T(8,128)} %bitcast.33), channel_id=1, source_target_pairs={{2,1},{6,5},{10,9},{14,13},{18,17},{22,21},{26,25},{30,29}} | collective-permute-start | bytes 3145736 | tf_op jit(solution)/shard_map/ppermute | solution.py:293
  954.4 128.1 %collective-permute-start.12 = (f32[64,2048]{1,0:T(8,128)}, f32[64,2048]{1,0:T(8,128)}, u32[]{:S(2)}, u32[]{:S(2)}) collective-permute-start(f32[64,2048]{1,0:T(8,128)} %bitcast.36), channel_id=1, source_target_pairs={{2,1},{6,5},{10,9},{14,13},{18,17},{22,21},{26,25},{30,29}} | collective-permute-start | bytes 1572872 | tf_op jit(solution)/shard_map/ppermute | solution.py:293
  999.4 83.1 %collective-permute-start.11 = (f32[64,2048]{1,0:T(8,128)}, f32[64,2048]{1,0:T(8,128)}, u32[]{:S(2)}, u32[]{:S(2)}) collective-permute-start(f32[64,2048]{1,0:T(8,128)} %bitcast.38), channel_id=1, source_target_pairs={{2,1},{6,5},{10,9},{14,13},{18,17},{22,21},{26,25},{30,29}} | collective-permute-start | bytes 1572872 | tf_op jit(solution)/shard_map/ppermute | solution.py:293
  1082.5 1.3 copy-start.2
Sparse Core Ops, SparseCore 0:
  383.0 145.4 reduce-scatter.13
  530.8 145.2 reduce-scatter.11
  678.4 111.3 reduce-scatter.9
  792.0 114.0 reduce-scatter.15
  908.2 46.1 reduce-scatter.19
  956.6 42.8 reduce-scatter.17
  1001.7 75.9 reduce-scatter.7

commit v2 on v1

--- a/solution.py
+++ b/solution.py
@@ -40,16 +40,26 @@
 def same_call(a, zs):
     rows, cols = a.shape
     q = rows // zs
-
-    def body(a_ref, o_ref):
-        mm(lambda ks: a_ref[:, ks], lambda ks: a_ref[:, ks], cols, o_ref.at[0])
+    h, e = q // 2, q // 4
+    wide = 10 * e
+
+    def body(a_ref, o_ref, left, right):
+        mm(lambda ks: a_ref[:, ks], lambda ks: a_ref[:h, ks], cols, left)
+        mm(lambda ks: a_ref[h:, ks], lambda ks: a_ref[h:, ks], cols, right)
+        o_ref[0, :, :e] = left[:e, :e]
+        o_ref[0, :, e : 3 * e] = left[e : 2 * e, :]
+        o_ref[0, :, 3 * e : 5 * e] = left[2 * e : 3 * e, :]
+        o_ref[0, :, 5 * e : 6 * e] = right[:e, :e]
+        o_ref[0, :, 6 * e : 8 * e] = left[3 * e :, :]
+        o_ref[0, :, 8 * e :] = right[e:, :]
 
     return pl.pallas_call(
         body,
         grid=(zs,),
         in_specs=[pl.BlockSpec((q, cols), lambda r: (r, 0))],
-        out_specs=pl.BlockSpec((1, q, q), lambda r: (r, 0, 0)),
-        out_shape=jax.ShapeDtypeStruct((zs, q, q), jnp.float32),
+        out_specs=pl.BlockSpec((1, e, wide), lambda r: (r, 0, 0)),
+        out_shape=jax.ShapeDtypeStruct((zs, e, wide), jnp.float32),
+        scratch_shapes=[pltpu.VMEM((q, h), jnp.float32), pltpu.VMEM((h, h), jnp.float32)],
         compiler_params=params(1),
         cost_estimate=cost(rows, q, cols),
         name="same_block",
@@ -152,7 +162,8 @@
 
 
 def own_call(zpos, same, low, up, far, far_other, rows):
-    q = same.shape[0]
+    q = low.shape[0]
+    e = q // 4
 
     def body(z_ref, same_ref, low_ref, up_ref, far_ref, other_ref, o_ref):
         z = z_ref[0]
@@ -160,7 +171,13 @@
         def cols(rel):
             return pl.ds(pl.multiple_of(((z + rel) % 4) * q, q), q)
 
-        o_ref[0, :, cols(0)] = same_ref[...]
+        for i in range(4):
+            for j in range(4):
+                hi, lo = max(i, j), min(i, j)
+                at = hi * (hi + 1) // 2 + lo
+                tile = same_ref[:, at * e : (at + 1) * e]
+                here = pl.ds(pl.multiple_of(z * q + j * e, e), e)
+                o_ref[0, i * e : (i + 1) * e, here] = tile if i >= j else tile.T
         o_ref[0, :, cols(1)] = up_ref[...].T
         o_ref[0, :, cols(3)] = low_ref[...]
 

time: 1100 us -> 1070 us (0.973)
  waiting for transfers between devices: 817 us -> 795 us
    reduce_scatter x7, waiting for transfers between devices: 313 us -> 288 us  [scatter(): return lax.psum_scatter(parts, 'kk', scatter_dimension=0, tiled=False)]
  transfers between devices with their start and end apart: 20 -> 20, of which waited for: 9 -> 9; matrix products, arithmetic and copies ran while one was open for 2% -> 2% of each run, Pallas kernels for 15% -> 16%
where the time goes in v2:
time: 1070 us
  waiting for transfers between devices  795 us (74%)
  Pallas kernels  223 us (21%)
  local copies, waits for them, and re-layouts  27.3 us (3%)
  starting transfers between devices  16 us (1%)
  between operations  13.6 us (1%)
    ppermute x5, waiting for transfers between devices, local_fn(): arrived[-1].append(lax.ppermute(piece, 'g', CROSS))  504 us
    reduce_scatter x7, waiting for transfers between devices, scatter(): return lax.psum_scatter(parts, 'kk', scatter_dimension=0, tiled=False)  288 us
    pallas_call x4, Pallas kernels, cross_call(): pl.pallas_call(body, grid_spec=pltpu.PrefetchScalarGridSpec(num_scalar_pr...  106 us
    pallas_call x1, Pallas kernels, rest_call(): pl.pallas_call(body, grid=(zs, 3), in_specs=[pl.BlockSpec((q, cols), left...  42.8 us
    pallas_call x1, Pallas kernels, near_call(): pl.pallas_call(body, grid=(rows // h,), in_specs=[pl.BlockSpec((zs, 1, h,...  41.8 us
  transfers between devices with their start and end apart: 20, of which 9 were waited for; matrix products, arithmetic and copies ran while one was open for 2% of the time, Pallas kernels for 16%

profile of v2, /device:TPU:0, one launch (start us, length us, event | category | flops | bytes accessed | tf_op | source)
XLA Modules:
  0.0 1074.4 jit_solution(7935641114086326817)
XLA Ops:
  6.5 0.5 collective-permute-start.2
  7.0 9.5 slice.31
  16.6 2.6 collective-permute-start.5
  19.2 7.8 fusion
  27.0 18.9 %same_block.1.dep_ref = f32[4,128,1280]{2,1,0:T(8,128)} custom-call(bf16[2048,7168]{1,0:T(8,128)(2,1)} %refs_1_.5), custom_call_target="tpu_custom_call" | custom-call | flops 15032385536 | bytes 40894464 | tf_op jit(solution)/shard_map/same_block/pallas_call | solution.py:56
  45.9 42.8 %rest_block.1 = f32[4,512,768]{2,1,0:T(8,128)} custom-call(bf16[2048,7168]{1,0:T(8,128)(2,1)} %refs_1_.5, bf16[2048,7168]{1,0:T(8,128)(2,1)} %refs_1_.5, f32[4,128,1280]{2,1,0:T(8,128)} %same_block.1.dep_ref), custom_call_target="tpu_custom_call" | custom-call | flops 22548578304 | bytes 46661632 | tf_op jit(solution)/shard_map/rest_block/pallas_call | solution.py:84
  88.7 41.8 %conditional.1 = (f32[1024,2048]{1,0:T(8,128)}) conditional(s32[]{:T(128)} %convert_element_type.3, (bf16[2048,7168]{1,0:T(8,128)(2,1)}, bf16[2048,7168]{1,0:T(8,128)(2,1)}, f32[4,512,768]{2,1,0:T(8,128)}) %tuple.11, (bf16[2048,7168]{1,0:T(8,128)(2,1)}, bf16[2048,7168]{1,0:T(8,128)(2,1)}, f32[4,512,768]{2,1,0:T(8,128)}) %tuple.12), branch_computations={%region_2.3_spmd, %region_3.4_spmd} | conditional | flops 30064771072 | bytes 52428808 | solution.py:293
  88.7 41.8 %near_block.3 = f32[1024,2048]{1,0:T(8,128)} custom-call(bf16[4,2,256,7168]{3,2,1,0:T(8,128)(2,1)} %bitcast.1.l_ref, bf16[2048,7168]{1,0:T(8,128)(2,1)} %get-tuple-element.24.r_ref, f32[4,512,768]{2,1,0:T(8,128)} %get-tuple-element.25.dep_ref), custom_call_target="tpu_custom_call" | custom-call | flops 30064771072 | bytes 52428800 | tf_op jit(solution)/shard_map/cond/branch_1_fun/near_block/pallas_call | solution.py:103
  130.5 204.8 %collective-permute-done.4.refs_0_ = bf16[256,7168]{1,0:T(8,128)(2,1)} collective-permute-done((bf16[256,7168]{1,0:T(8,128)(2,1)}, bf16[256,7168]{1,0:T(8,128)(2,1)}, u32[]{:S(2)}, u32[]{:S(2)}) %collective-permute-start.4) | collective-permute-done | bytes 3670048 | tf_op jit(solution)/shard_map/ppermute | solution.py:282
  335.3 47.5 %cross_block.4.refs_2_ = f32[4,256,2048]{2,1,0:T(8,128)} custom-call(s32[1]{0:T(128)} %bitcast.2.pos_ref.p_ref, bf16[256,7168]{1,0:T(8,128)(2,1)} %collective-permute-done.4.refs_0_, bf16[768,7168]{1,0:T(8,128)(2,1)} %collective-permute-done.5.refs_1_, bf16[2048,7168]{1,0:T(8,128)(2,1)} %refs_1_.5, f32[1024,2048]{1,0:T(8,128)} %get-tuple-element.29.refs_3_), custom_call_target="tpu_custom_call" | custom-call | flops 30064771072 | bytes 52428800 | tf_op jit(solution)/shard_map/cross_block/pallas_call | solution.py:147
  382.9 0.0 reduce-scatter.12.cloned.1.call-start
  382.9 0.7 reduce-scatter.12.cloned.1.call-update
  383.6 0.0 reduce-scatter.10.cloned.1.call-start
  383.7 0.7 reduce-scatter.10.cloned.1.call-update
  384.4 0.0 reduce-scatter.16.cloned.1.call-start
  384.4 3.6 slice.32
  388.0 1.3 collective-permute-start.6
  389.3 158.8 %collective-permute-done.6.refs_0_ = bf16[512,7168]{1,0:T(8,128)(2,1)} collective-permute-done((bf16[512,7168]{1,0:T(8,128)(2,1)S(1)}, bf16[512,7168]{1,0:T(8,128)(2,1)}, u32[]{:S(2)}, u32[]{:S(2)}) %collective-permute-start.6) | collective-permute-done | bytes 7340064 | tf_op jit(solution)/shard_map/ppermute | solution.py:282
  548.1 25.7 %cross_block.5.refs_2_ = f32[4,128,2048]{2,1,0:T(8,128)} custom-call(s32[1]{0:T(128)} %bitcast.2.pos_ref.p_ref, bf16[512,7168]{1,0:T(8,128)(2,1)} %collective-permute-done.6.refs_0_, bf16[2048,7168]{1,0:T(8,128)(2,1)} %refs_1_.5, f32[4,256,2048]{2,1,0:T(8,128)} %cross_block.4.refs_2_), custom_call_target="tpu_custom_call" | custom-call | flops 15032385536 | bytes 40894464 | tf_op jit(solution)/shard_map/cross_block/pallas_call | solution.py:147
  573.9 0.0 reduce-scatter.20.cloned.1.call-start
  573.9 1.2 collective-permute-start.7
  575.2 0.1 collective-permute-start.8
  575.2 81.2 %collective-permute-done.7.refs_0_ = bf16[256,7168]{1,0:T(8,128)(2,1)S(1)} collective-permute-done((bf16[256,7168]{1,0:T(8,128)(2,1)}, bf16[256,7168]{1,0:T(8,128)(2,1)S(1)}, u32[]{:S(2)}, u32[]{:S(2)}) %collective-permute-start.7) | collective-permute-done | bytes 3670048 | tf_op jit(solution)/shard_map/ppermute | solution.py:282
  656.4 1.8 copy-done.1
  658.2 16.5 %cross_block.6.refs_2_ = f32[4,64,2048]{2,1,0:T(8,128)} custom-call(s32[1]{0:T(128)} %bitcast.2.pos_ref.p_ref, bf16[256,7168]{1,0:T(8,128)(2,1)} %copy-done.1, bf16[2048,7168]{1,0:T(8,128)(2,1)} %refs_1_.5, f32[4,128,2048]{2,1,0:T(8,128)} %cross_block.5.refs_2_), custom_call_target="tpu_custom_call" | custom-call | flops 7516192768 | bytes 35127296 | tf_op jit(solution)/shard_map/cross_block/pallas_call | solution.py:147
  674.7 59.3 %collective-permute-done.8.refs_0_ = bf16[256,7168]{1,0:T(8,128)(2,1)} collective-permute-done((bf16[256,7168]{1,0:T(8,128)(2,1)}, bf16[256,7168]{1,0:T(8,128)(2,1)}, u32[]{:S(2)}, u32[]{:S(2)}) %collective-permute-start.8) | collective-permute-done | bytes 3670048 | tf_op jit(solution)/shard_map/ppermute | solution.py:282
  734.0 16.6 %cross_block.7 = f32[4,64,2048]{2,1,0:T(8,128)} custom-call(s32[1]{0:T(128)} %bitcast.2.pos_ref.p_ref, bf16[256,7168]{1,0:T(8,128)(2,1)} %collective-permute-done.8.refs_0_, bf16[2048,7168]{1,0:T(8,128)(2,1)} %refs_1_.5, f32[4,64,2048]{2,1,0:T(8,128)} %cross_block.6.refs_2_), custom_call_target="tpu_custom_call" | custom-call | flops 7516192768 | bytes 35127296 | tf_op jit(solution)/shard_map/cross_block/pallas_call | solution.py:147
  750.6 0.0 reduce-scatter.18.cloned.1.call-start
  750.7 0.5 reduce-scatter.18.cloned.1.call-update
  751.2 0.0 reduce-scatter.8.cloned.1.call-start
  751.3 0.7 reduce-scatter.8.cloned.1.call-update
  752.0 0.8 collective-permute-start.9
  752.8 1.3 collective-permute-start.3
  754.1 35.7 %reduce-scatter.10.cloned.1.call-done = f32[1,512,768]{2,1,0:T(8,128)} async-done(((f32[4,512,768]{2,1,0:T(8,128)}), f32[1,512,768]{2,1,0:T(8,128)}) %reduce-scatter.10.cloned.1.call-update) | async-done | bytes 1572880 | tf_op jit(solution)/shard_map/reduce_scatter | solution.py:265
  789.8 1.3 slice.28.low_ref
  791.1 2.7 collective-permute-start
  793.8 1.9 slice.29.far_ref
  795.7 0.7 collective-permute-start.1
  796.3 109.8 %reduce-scatter.16.cloned.1.call-done = f32[1,128,2048]{2,1,0:T(8,128)} async-done(((f32[4,128,2048]{2,1,0:T(8,128)}), f32[1,128,2048]{2,1,0:T(8,128)}) %reduce-scatter.16.cloned.1.call-update) | async-done | bytes 1048592 | tf_op jit(solution)/shard_map/reduce_scatter | solution.py:265
  906.1 1.6 collective-permute-start.10
  907.8 46.7 %reduce-scatter.20.cloned.1.call-done = f32[1,64,2048]{2,1,0:T(8,128)} async-done(((f32[4,64,2048]{2,1,0:T(8,128)}), f32[1,64,2048]{2,1,0:T(8,128)}) %reduce-scatter.20.cloned.1.call-update) | async-done | bytes 524304 | tf_op jit(solution)/shard_map/reduce_scatter | solution.py:265
  954.4 1.5 collective-permute-start.12
  955.9 43.5 %reduce-scatter.18.cloned.1.call-done = f32[1,64,2048]{2,1,0:T(8,128)} async-done(((f32[4,64,2048]{2,1,0:T(8,128)}), f32[1,64,2048]{2,1,0:T(8,128)}) %reduce-scatter.18.cloned.1.call-update) | async-done | bytes 524304 | tf_op jit(solution)/shard_map/reduce_scatter | solution.py:265
  999.4 1.4 collective-permute-start.11
  1000.9 52.4 %reduce-scatter.8.cloned.1.call-done = f32[1,128,1280]{2,1,0:T(8,128)} async-done(((f32[4,128,1280]{2,1,0:T(8,128)}), f32[1,128,1280]{2,1,0:T(8,128)}) %reduce-scatter.8.cloned.1.call-update) | async-done | bytes 655376 | tf_op jit(solution)/shard_map/reduce_scatter | solution.py:265
  1053.2 4.7 own_out.1.out_ref
  1058.0 1.3 copy-done.2
  1059.3 8.2 slots_out.1
  (20 shorter events, 0.1 us)
Async XLA Ops:
  6.5 745.4 %reduce-scatter.14.cloned.1.call-start = ((), (), s32[]{:S(2)}) async-start(), calls=%async_computation.10 | async-start | bytes 10485760 | tf_op jit(solution)/shard_map/reduce_scatter | solution.py:265
  6.5 82.2 %collective-permute-start.2 = (bf16[2048,7168]{1,0:T(8,128)(2,1)}, bf16[2048,7168]{1,0:T(8,128)(2,1)}, u32[]{:S(2)}, u32[]{:S(2)}) collective-permute-start(bf16[2048,7168]{1,0:T(8,128)(2,1)} %refs_1_.5), channel_id=1, source_target_pairs={{0,1},{1,0},{2,3},{3,2},{4,5},{5,4},{6,7},{7,6},{8,9},{9,8},{10,11... | collective-permute-start | bytes 88080392 | tf_op jit(solution)/shard_map/ppermute | solution.py:285
  16.6 318.8 %collective-permute-start.5 = (bf16[768,7168]{1,0:T(8,128)(2,1)}, bf16[768,7168]{1,0:T(8,128)(2,1)}, u32[]{:S(2)}, u32[]{:S(2)}) collective-permute-start(bf16[768,7168]{1,0:T(8,128)(2,1)} %bitcast.10), channel_id=1, source_target_pairs={{0,3},{1,2},{2,0},{3,1},{4,7},{5,6},{6,4},{7,5},{8,11},{9,10},{10,... | collective-permute-start | bytes 33030152 | tf_op jit(solution)/shard_map/ppermute | solution.py:282
  27.0 308.3 %collective-permute-start.4 = (bf16[256,7168]{1,0:T(8,128)(2,1)}, bf16[256,7168]{1,0:T(8,128)(2,1)}, u32[]{:S(2)}, u32[]{:S(2)}) collective-permute-start(bf16[256,7168]{1,0:T(8,128)(2,1)} %bitcast.9), channel_id=1, source_target_pairs={{0,3},{1,2},{2,0},{3,1},{4,7},{5,6},{6,4},{7,5},{8,11},{9,10},{10,... | collective-permute-start | bytes 11010056 | tf_op jit(solution)/shard_map/ppermute | solution.py:282
  382.9 369.9 %reduce-scatter.12.cloned.1.call-start = ((), (), s32[]{:S(2)}) async-start(), calls=%async_computation.9 | async-start | bytes 10485760 | tf_op jit(solution)/shard_map/reduce_scatter | solution.py:265
  383.6 406.2 %reduce-scatter.10.cloned.1.call-start = ((), (), s32[]{:S(2)}) async-start(), calls=%async_computation.8 | async-start | bytes 7864320 | tf_op jit(solution)/shard_map/reduce_scatter | solution.py:265
  384.4 521.7 %reduce-scatter.16.cloned.1.call-start = ((), (), s32[]{:S(2)}) async-start(), calls=%async_computation.11 | async-start | bytes 5242880 | tf_op jit(solution)/shard_map/reduce_scatter | solution.py:265
  388.0 160.2 %collective-permute-start.6 = (bf16[512,7168]{1,0:T(8,128)(2,1)S(1)}, bf16[512,7168]{1,0:T(8,128)(2,1)}, u32[]{:S(2)}, u32[]{:S(2)}) collective-permute-start(bf16[512,7168]{1,0:T(8,128)(2,1)S(1)} %bitcast.24), channel_id=1, source_target_pairs={{0,3},{1,2},{2,0},{3,1},{4,7},{5,6},{6,4},{7,5},{8,11},{9,10},{10,... | collective-permute-start | bytes 22020104 | tf_op jit(solution)/shard_map/ppermute | solution.py:282
  573.9 380.6 %reduce-scatter.20.cloned.1.call-start = ((), (), s32[]{:S(2)}) async-start(), calls=%async_computation.13 | async-start | bytes 2621440 | tf_op jit(solution)/shard_map/reduce_scatter | solution.py:265
  573.9 82.5 %collective-permute-start.7 = (bf16[256,7168]{1,0:T(8,128)(2,1)}, bf16[256,7168]{1,0:T(8,128)(2,1)S(1)}, u32[]{:S(2)}, u32[]{:S(2)}) collective-permute-start(bf16[256,7168]{1,0:T(8,128)(2,1)} %bitcast.26), channel_id=1, source_target_pairs={{0,3},{1,2},{2,0},{3,1},{4,7},{5,6},{6,4},{7,5},{8,11},{9,10},{10,... | collective-permute-start | bytes 11010056 | tf_op jit(solution)/shard_map/ppermute | solution.py:282
  575.2 158.9 %collective-permute-start.8 = (bf16[256,7168]{1,0:T(8,128)(2,1)}, bf16[256,7168]{1,0:T(8,128)(2,1)}, u32[]{:S(2)}, u32[]{:S(2)}) collective-permute-start(bf16[256,7168]{1,0:T(8,128)(2,1)} %bitcast.25), channel_id=1, source_target_pairs={{0,3},{1,2},{2,0},{3,1},{4,7},{5,6},{6,4},{7,5},{8,11},{9,10},{10,... | collective-permute-start | bytes 11010056 | tf_op jit(solution)/shard_map/ppermute | solution.py:282
  656.4 1.8 copy-start.1
  750.6 248.8 %reduce-scatter.18.cloned.1.call-start = ((), (), s32[]{:S(2)}) async-start(), calls=%async_computation.12 | async-start | bytes 2621440 | tf_op jit(solution)/shard_map/reduce_scatter | solution.py:265
  751.2 302.0 %reduce-scatter.8.cloned.1.call-start = ((), (), s32[]{:S(2)}) async-start(), calls=%async_computation.7 | async-start | bytes 3276800 | tf_op jit(solution)/shard_map/reduce_scatter | solution.py:265
  752.0 306.0 %collective-permute-start.9 = (f32[256,2048]{1,0:T(8,128)}, f32[256,2048]{1,0:T(8,128)S(1)}, u32[]{:S(2)}, u32[]{:S(2)}) collective-permute-start(f32[256,2048]{1,0:T(8,128)} %bitcast.27), channel_id=1, source_target_pairs={{2,1},{6,5},{10,9},{14,13},{18,17},{22,21},{26,25},{30,29}} | collective-permute-start | bytes 6291464 | tf_op jit(solution)/shard_map/ppermute | solution.py:310
  752.8 305.2 %collective-permute-start.3 = (f32[256,2048]{1,0:T(8,128)}, f32[256,2048]{1,0:T(8,128)}, u32[]{:S(2)}, u32[]{:S(2)}) collective-permute-start(f32[256,2048]{1,0:T(8,128)} %bitcast.29), channel_id=1, source_target_pairs={{1,0},{3,2},{5,4},{7,6},{9,8},{11,10},{13,12},{15,14},{17,16},{19,... | collective-permute-start | bytes 6291464 | tf_op jit(solution)/shard_map/ppermute | solution.py:308
  791.1 262.1 %copy-start = (f32[512,512]{1,0:T(8,128)}, f32[512,512]{1,0:T(8,128)S(1)}, u32[]{:S(2)}) copy-start(f32[512,512]{1,0:T(8,128)S(1)} %slice.28.low_ref) | copy-start | bytes 3145732
  791.1 164.8 %collective-permute-start = (f32[512,512]{1,0:T(8,128)S(1)}, f32[512,512]{1,0:T(8,128)}, u32[]{:S(2)}, u32[]{:S(2)}) collective-permute-start(f32[512,512]{1,0:T(8,128)S(1)} %slice.28.low_ref), channel_id=1, source_target_pairs={{0,12},{4,0},{8,4},{12,8},{1,13},{5,1},{9,5},{13,9},{2,14},{6,2},{... | collective-permute-start | bytes 3145736 | tf_op jit(solution)/shard_map/ppermute | solution.py:306
  795.7 112.1 %collective-permute-start.1 = (f32[512,256]{1,0:T(8,128)}, f32[512,256]{1,0:T(8,128)}, u32[]{:S(2)}, u32[]{:S(2)}) collective-permute-start(f32[512,256]{1,0:T(8,128)} %slice.29.far_ref), channel_id=1, source_target_pairs={{0,8},{4,12},{8,0},{12,4},{1,9},{5,13},{9,1},{13,5},{2,10},{6,14},... | collective-permute-start | bytes 1572872 | tf_op jit(solution)/shard_map/ppermute | solution.py:307
  906.1 151.9 %collective-permute-start.10 = (f32[128,2048]{1,0:T(8,128)}, f32[128,2048]{1,0:T(8,128)}, u32[]{:S(2)}, u32[]{:S(2)}) collective-permute-start(f32[128,2048]{1,0:T(8,128)} %bitcast.33), channel_id=1, source_target_pairs={{2,1},{6,5},{10,9},{14,13},{18,17},{22,21},{26,25},{30,29}} | collective-permute-start | bytes 3145736 | tf_op jit(solution)/shard_map/ppermute | solution.py:310
  954.4 103.5 %collective-permute-start.12 = (f32[64,2048]{1,0:T(8,128)}, f32[64,2048]{1,0:T(8,128)}, u32[]{:S(2)}, u32[]{:S(2)}) collective-permute-start(f32[64,2048]{1,0:T(8,128)} %bitcast.36), channel_id=1, source_target_pairs={{2,1},{6,5},{10,9},{14,13},{18,17},{22,21},{26,25},{30,29}} | collective-permute-start | bytes 1572872 | tf_op jit(solution)/shard_map/ppermute | solution.py:310
  999.4 58.5 %collective-permute-start.11 = (f32[64,2048]{1,0:T(8,128)}, f32[64,2048]{1,0:T(8,128)}, u32[]{:S(2)}, u32[]{:S(2)}) collective-permute-start(f32[64,2048]{1,0:T(8,128)} %bitcast.38), channel_id=1, source_target_pairs={{2,1},{6,5},{10,9},{14,13},{18,17},{22,21},{26,25},{30,29}} | collective-permute-start | bytes 1572872 | tf_op jit(solution)/shard_map/ppermute | solution.py:310
  1058.0 1.3 copy-start.2
Sparse Core Ops, SparseCore 0:
  383.0 145.4 reduce-scatter.13
  530.8 145.1 reduce-scatter.11
  678.4 111.3 reduce-scatter.9
  792.0 114.1 reduce-scatter.15
  908.3 46.1 reduce-scatter.19
  956.6 42.8 reduce-scatter.17
  1001.7 51.4 reduce-scatter.7
